TPU v7x, 32 devices: a whole 2x2x4 slice. The times are simulated.
32 devices in a mesh: expert: 2 (over x), batch: 4 (over z), seq: 4 (over y, core).
Axes of the slice: x: 2, y: 2, z: 4, core: 2. Of those that a mesh axis runs over, the one named last changes fastest.
Arguments:
- queries: bfloat16 [2, 4, 2, 384, 4096], P('expert', 'batch', None, 'seq'), may hold values from -36 to 36
- keys: bfloat16 [2, 4, 2, 384, 4096], P('expert', 'batch', None, 'seq'), may hold values from -21 to 21
- values: bfloat16 [2, 4, 2, 384, 4096], P('expert', 'batch', None, 'seq'), may hold values from -6 to 6
- latents: bfloat16 [2, 4, 384, 4096], P('expert', 'batch', 'seq'), may hold values from -6 to 6
- gain: bfloat16 [2, 4096], P('expert'), may hold values from 0.099609375 to 1.8984375
- steps_table: int32 [2, 4], P('expert', 'batch'), may hold values from 0 to 38
- flags: int32 [4], P('batch'), may hold values 0 or 1
Outputs:
- denoised: bfloat16 [2, 4, 384, 4096], P('expert', 'batch', 'seq')
- next_latents: bfloat16 [2, 4, 384, 4096], P('expert', 'batch', 'seq')
All inputs are finite; a program needn't handle non-finite values. No bound on the sum of `flags` on one device may be relied on, other than what follows from the above.
Results may differ from a plain program's by a relative error of at most 0.006.
Values may be sent and summed in bfloat16 or wider, within the bound.
A program may use at most 64 MiB of HBM per device.

v0:
```python
import jax
import jax.numpy as jnp
from jax import lax
from jax.sharding import PartitionSpec as P

HDIM = 128
STEPS = 40
GUIDANCE = 3.5
flow_shift = 5.0


def from_partner(block, axis, bit):
    count = lax.axis_size(axis)
    route = []
    for low in range(count):
        high = low | 1 << bit
        if high != low and high < count:
            route += [(low, high), (high, low)]
    return lax.ppermute(block, axis, route)


def sigma_of(step):
    level = 1.0 - step.astype(jnp.float32) / STEPS
    return flow_shift * level / (1.0 + (flow_shift - 1.0) * level)


def combine(cond, uncond):
    base = uncond.astype(jnp.float32)
    return (base + GUIDANCE * (cond.astype(jnp.float32) - base)).astype(jnp.bfloat16)


def attend(stacked):
    query_heads, key_heads, value_heads = stacked
    items, length, width_dev = query_heads.shape
    heads_dev = width_dev // HDIM
    block = 512 if length % 512 == 0 else length
    key_rows = key_heads.reshape(items, length, heads_dev, HDIM)
    value_rows = value_heads.reshape(items, length, heads_dev, HDIM)
    query_blocks = query_heads.reshape(items, length // block, block, heads_dev, HDIM).transpose(
        1, 0, 2, 3, 4
    )

    def one_block(query_part):
        scores = jnp.einsum(
            "nqhd,nkhd->nhqk", query_part, key_rows, preferred_element_type=jnp.float32
        ) * HDIM ** (-0.5)
        weights = jax.nn.softmax(scores, axis=-1).astype(jnp.bfloat16)
        return jnp.einsum(
            "nhqk,nkhd->nqhd", weights, value_rows, preferred_element_type=jnp.float32
        ).astype(jnp.bfloat16)

    result = lax.map(one_block, query_blocks)
    return result.transpose(1, 0, 2, 3, 4).reshape(items, length, width_dev)


def per_device(queries, keys, values, latents, gain, steps_table, flags):
    attended = attend(
        (
            lax.all_to_all(queries[0, 0], "seq", split_axis=2, concat_axis=1, tiled=True),
            lax.all_to_all(keys[0, 0], "seq", split_axis=2, concat_axis=1, tiled=True),
            lax.all_to_all(values[0, 0], "seq", split_axis=2, concat_axis=1, tiled=True),
        )
    )
    guided = lax.all_to_all(
        combine(attended[0], attended[1]), "seq", split_axis=0, concat_axis=1, tiled=True
    )
    guided_f32 = guided.astype(jnp.float32)
    scale = lax.rsqrt(jnp.mean(guided_f32 * guided_f32, axis=-1, keepdims=True) + 1e-06)
    velocity = guided_f32 * scale * gain[0].astype(jnp.float32)[None, :]
    step_now = steps_table[0, 0]
    sigma_now = sigma_of(step_now)
    sigma_next = sigma_of(step_now + 1)
    current = latents[0, 0].astype(jnp.float32)
    denoised = (current - sigma_now * velocity).astype(jnp.bfloat16)
    moved = (current + (sigma_next - sigma_now) * velocity).astype(jnp.bfloat16)
    partner = from_partner(moved, "expert", 0)
    next_latents = jnp.where(flags[0] == 1, partner, moved)
    return (denoised[None, None], next_latents[None, None])


def solution(mesh):
    placed = (
        P("expert", "batch", None, "seq", None),
        P("expert", "batch", None, "seq", None),
        P("expert", "batch", None, "seq", None),
        P("expert", "batch", "seq", None),
        P("expert", None),
        P("expert", "batch"),
        P("batch"),
    )
    return jax.shard_map(
        per_device,
        mesh=mesh,
        in_specs=placed,
        out_specs=(P("expert", "batch", "seq", None), P("expert", "batch", "seq", None)),
        check_vma=False,
    )
```

profile of v0, /device:TPU:0, one launch (start us, length us, event | category | flops | bytes accessed | tf_op | source)
XLA Modules:
  0.0 159.6 jit_solution(14842761862056379476)
XLA Ops:
  0.6 5.7 %copy.30 = bf16[1,1,2,96,4096]{3,2,4,1,0:T(2,128)(2,1)} copy(bf16[1,1,2,96,4096]{4,3,2,1,0:T(8,128)(2,1)} %param.7) | data formatting | bytes 3145728 | tf_op args[0]
  6.3 4.3 %all-to-all-start = ((bf16[2,96,4096]{1,0,2:T(2,128)(2,1)}), bf16[2,96,4096]{1,0,2:T(2,128)(2,1)S(1)}, u32[]{:S(2)}, u32[]{:S(2)}) async-start(bf16[2,96,4096]{1,0,2:T(2,128)(2,1)} %bitcast.50), calls=%async_computation | async-start | bytes 4194304 | tf_op jit(solution)/shard_map/all_to_all | solution.py:59
  10.6 5.7 %copy.32 = bf16[1,1,2,96,4096]{3,2,4,1,0:T(2,128)(2,1)} copy(bf16[1,1,2,96,4096]{4,3,2,1,0:T(8,128)(2,1)} %param.8) | data formatting | bytes 3145728 | tf_op args[1]
  16.3 20.0 %all-to-all-done = bf16[2,96,4096]{1,0,2:T(2,128)(2,1)S(1)} async-done(((bf16[2,96,4096]{1,0,2:T(2,128)(2,1)}), bf16[2,96,4096]{1,0,2:T(2,128)(2,1)S(1)}, u32[]{:S(2)}, u32[]{:S(2)}) %all-to-all-start) | async-done | bytes 1572896 | tf_op jit(solution)/shard_map/all_to_all | solution.py:59
  36.3 4.4 %all-to-all-start.1 = ((bf16[2,96,4096]{1,0,2:T(2,128)(2,1)}), bf16[2,96,4096]{1,0,2:T(2,128)(2,1)}, u32[]{:S(2)}, u32[]{:S(2)}) async-start(bf16[2,96,4096]{1,0,2:T(2,128)(2,1)} %bitcast.49), calls=%async_computation.1 | async-start | bytes 4194304 | tf_op jit(solution)/shard_map/all_to_all | solution.py:60
  40.7 5.7 %copy.36 = bf16[1,1,2,96,4096]{3,2,4,1,0:T(2,128)(2,1)} copy(bf16[1,1,2,96,4096]{4,3,2,1,0:T(8,128)(2,1)} %param.9) | data formatting | bytes 3145728 | tf_op args[2]
  46.4 20.0 %all-to-all-done.1 = bf16[2,96,4096]{1,0,2:T(2,128)(2,1)} async-done(((bf16[2,96,4096]{1,0,2:T(2,128)(2,1)}), bf16[2,96,4096]{1,0,2:T(2,128)(2,1)}, u32[]{:S(2)}, u32[]{:S(2)}) %all-to-all-start.1) | async-done | bytes 1572896 | tf_op jit(solution)/shard_map/all_to_all | solution.py:60
  66.4 4.4 %all-to-all-start.2 = ((bf16[2,96,4096]{1,0,2:T(2,128)(2,1)}), bf16[2,96,4096]{1,0,2:T(2,128)(2,1)}, u32[]{:S(2)}, u32[]{:S(2)}) async-start(bf16[2,96,4096]{1,0,2:T(2,128)(2,1)} %bitcast.48), calls=%async_computation.2 | async-start | bytes 4194304 | tf_op jit(solution)/shard_map/all_to_all | solution.py:61
  70.9 3.7 %copy.31 = bf16[2,96,4,1024]{3,1,2,0:T(8,128)(2,1)} copy(bf16[2,96,4,1024]{1,0,3,2:T(2,128)(2,1)S(1)} %bitcast.47) | data formatting | bytes 3145728 | tf_op jit(solution)/shard_map/all_to_all | solution.py:59
  74.6 1.8 %copy.46 = bf16[96,8,8,128]{3,2,1,0:T(8,128)(2,1)S(1)} copy(bf16[96,8,8,128]{3,1,2,0:T(8,128)(2,1)} %bitcast.54) | data formatting | bytes 3145728
  76.4 4.7 %copy.33 = bf16[2,96,4,1024]{3,1,2,0:T(8,128)(2,1)S(1)} copy(bf16[2,96,4,1024]{1,0,3,2:T(2,128)(2,1)} %bitcast.5) | data formatting | bytes 3145728 | tf_op jit(solution)/shard_map/all_to_all | solution.py:60
  81.6 1.4 fusion.12
  83.0 3.6 %copy-done = f32[2,8,384,384]{2,3,1,0:T(8,128)} copy-done((f32[2,8,384,384]{2,3,1,0:T(8,128)}, f32[2,8,384,384]{2,3,1,0:T(8,128)S(1)}, u32[]{:S(2)}) %copy-start) | copy-done | bytes 9437208
  86.6 2.4 %fusion.26 = f32[2,8,384]{2,1,0:T(8,128)S(1)} fusion(f32[2,8,384,384]{2,3,1,0:T(8,128)S(1)} %fusion.12), kind=kOutput, calls=%fused_computation.30 | output fusion | flops 9437567 | bytes 9461760 | tf_op jit(solution)/shard_map/while/body/eval_jaxpr/sub | solution.py:47
  89.0 7.6 %all-to-all-done.2 = bf16[2,96,4096]{1,0,2:T(2,128)(2,1)} async-done(((bf16[2,96,4096]{1,0,2:T(2,128)(2,1)}), bf16[2,96,4096]{1,0,2:T(2,128)(2,1)}, u32[]{:S(2)}, u32[]{:S(2)}) %all-to-all-start.2) | async-done | bytes 1572896 | tf_op jit(solution)/shard_map/all_to_all | solution.py:61
  96.6 4.7 %copy.37 = bf16[2,96,4,1024]{3,1,2,0:T(8,128)(2,1)S(1)} copy(bf16[2,96,4,1024]{1,0,3,2:T(2,128)(2,1)} %bitcast.8) | data formatting | bytes 3145728 | tf_op jit(solution)/shard_map/all_to_all | solution.py:61
  101.7 9.9 %fusion.15 = bf16[2,384,8,128]{3,1,2,0:T(8,128)(2,1)S(1)} fusion(bf16[2,384,8,128]{3,2,1,0:T(8,128)(2,1)S(1)} %bitcast.57, f32[2,8,384]{2,1,0:T(8,128)S(1)} %fusion.26, f32[2,8,384,384]{2,3,1,0:T(8,128)} %copy-done), kind=kOutput, calls=%fused_computation.22 | convolution fusion | flops 616569216 | bytes 12607488 | tf_op jit(solution)/shard_map/while/body/eval_jaxpr/nhqk,nkhd->nqhd/dot_general | solution.py:48
  111.9 0.9 copy.40
  112.8 1.4 reshape.129
  114.2 0.9 copy.41
  115.1 1.4 reshape.130
  117.0 2.6 %add_convert_fusion = bf16[4,96,1024]{2,1,0:T(8,128)(2,1)} fusion(f32[4,96,1024]{2,1,0:T(8,128)S(1)} %copy-done.1, f32[4,96,1024]{2,1,0:T(8,128)} %reshape.130), kind=kLoop, calls=%fused_computation.21 | loop fusion | flops 1572864 | bytes 3932160 | tf_op jit(solution)/shard_map/convert_element_type | solution.py:29
  119.7 3.8 %all-to-all-start.3 = ((bf16[4,96,1024]{2,1,0:T(8,128)(2,1)}), bf16[4,96,1024]{2,1,0:T(8,128)(2,1)S(1)}, u32[]{:S(2)}, u32[]{:S(2)}) async-start(bf16[4,96,1024]{2,1,0:T(8,128)(2,1)} %add_convert_fusion), calls=%async_computation.3 | async-start | bytes 1572864 | tf_op jit(solution)/shard_map/all_to_all | solution.py:64
  124.9 10.0 %all-to-all-done.3 = bf16[4,96,1024]{2,1,0:T(8,128)(2,1)S(1)} async-done(((bf16[4,96,1024]{2,1,0:T(8,128)(2,1)}), bf16[4,96,1024]{2,1,0:T(8,128)(2,1)S(1)}, u32[]{:S(2)}, u32[]{:S(2)}) %all-to-all-start.3) | async-done | bytes 786464 | tf_op jit(solution)/shard_map/all_to_all | solution.py:64
  135.7 0.8 copy-done.2
  136.4 1.2 fusion.9
  137.7 2.3 %collective-permute-start = (bf16[96,4096]{1,0:T(8,128)(2,1)}, bf16[96,4096]{1,0:T(8,128)(2,1)}, u32[]{:S(2)}, u32[]{:S(2)}) collective-permute-start(bf16[96,4096]{1,0:T(8,128)(2,1)} %fusion.9), channel_id=1, source_target_pairs={{0,16},{16,0},{1,17},{17,1},{2,18},{18,2},{3,19},{19,3},{4,20},{20... | collective-permute-start | bytes 2359304 | tf_op jit(solution)/shard_map/ppermute | solution.py:19
  139.9 1.0 copy.42
  141.0 1.1 reshape.131
  142.0 2.4 %fusion.7 = bf16[1,1,96,4096]{3,2,1,0:T(8,128)(2,1)} fusion(bf16[1,1,96,4096]{3,2,1,0:T(8,128)(2,1)} %param.10, f32[1,1,96,4096]{3,2,1,0:T(8,128)S(1)} %reshape.131, f32[4096]{0:T(1024)S(1)} %bitcast.59, f32[96]{0:T(128)S(1)} %add_rsqrt_fusion, f32[]{:T(128)} %bitcast), kind=kLoop, calls=%fused_computation.13 | loop fusion | flops 2359296 | bytes 3162500 | tf_op jit(solution)/shard_map/convert_element_type | solution.py:74
  144.4 13.1 %collective-permute-done = bf16[96,4096]{1,0:T(8,128)(2,1)} collective-permute-done((bf16[96,4096]{1,0:T(8,128)(2,1)}, bf16[96,4096]{1,0:T(8,128)(2,1)}, u32[]{:S(2)}, u32[]{:S(2)}) %collective-permute-start) | collective-permute-done | bytes 786464 | tf_op jit(solution)/shard_map/ppermute | solution.py:19
  157.5 2.1 %select_bitcast_fusion = bf16[1,1,96,4096]{3,2,1,0:T(8,128)(2,1)} fusion(bf16[96,4096]{1,0:T(8,128)(2,1)} %collective-permute-done, bf16[96,4096]{1,0:T(8,128)(2,1)} %fusion.9, pred[]{:T(512)} %bitcast.13), kind=kLoop, calls=%fused_computation.25 | loop fusion | flops 393216 | bytes 2359297 | tf_op jit(solution)/shard_map/broadcast_in_dim | solution.py:78
  (14 shorter events, 2.4 us)
Async XLA Ops:
  6.3 29.9 %all-to-all-start = ((bf16[2,96,4096]{1,0,2:T(2,128)(2,1)}), bf16[2,96,4096]{1,0,2:T(2,128)(2,1)S(1)}, u32[]{:S(2)}, u32[]{:S(2)}) async-start(bf16[2,96,4096]{1,0,2:T(2,128)(2,1)} %bitcast.50), calls=%async_computation | async-start | bytes 4194304 | tf_op jit(solution)/shard_map/all_to_all | solution.py:59
  36.3 30.2 %all-to-all-start.1 = ((bf16[2,96,4096]{1,0,2:T(2,128)(2,1)}), bf16[2,96,4096]{1,0,2:T(2,128)(2,1)}, u32[]{:S(2)}, u32[]{:S(2)}) async-start(bf16[2,96,4096]{1,0,2:T(2,128)(2,1)} %bitcast.49), calls=%async_computation.1 | async-start | bytes 4194304 | tf_op jit(solution)/shard_map/all_to_all | solution.py:60
  66.4 30.2 %all-to-all-start.2 = ((bf16[2,96,4096]{1,0,2:T(2,128)(2,1)}), bf16[2,96,4096]{1,0,2:T(2,128)(2,1)}, u32[]{:S(2)}, u32[]{:S(2)}) async-start(bf16[2,96,4096]{1,0,2:T(2,128)(2,1)} %bitcast.48), calls=%async_computation.2 | async-start | bytes 4194304 | tf_op jit(solution)/shard_map/all_to_all | solution.py:61
  83.0 3.6 %copy-start = (f32[2,8,384,384]{2,3,1,0:T(8,128)}, f32[2,8,384,384]{2,3,1,0:T(8,128)S(1)}, u32[]{:S(2)}) copy-start(f32[2,8,384,384]{2,3,1,0:T(8,128)S(1)} %fusion.12) | copy-start | bytes 28311556
  115.1 1.9 %copy-start.1 = (f32[4,96,1024]{2,1,0:T(8,128)S(1)}, f32[4,96,1024]{2,1,0:T(8,128)}, u32[]{:S(2)}) copy-start(f32[4,96,1024]{2,1,0:T(8,128)} %reshape.129) | copy-start | bytes 4718596
  119.7 4.5 %copy-start.3 = (bf16[1,4096]{1,0:T(2,128)(2,1)S(1)}, bf16[1,4096]{1,0:T(2,128)(2,1)}, u32[]{:S(2)}) copy-start(bf16[1,4096]{1,0:T(2,128)(2,1)} %param.11) | copy-start | bytes 24580
  119.7 15.2 %all-to-all-start.3 = ((bf16[4,96,1024]{2,1,0:T(8,128)(2,1)}), bf16[4,96,1024]{2,1,0:T(8,128)(2,1)S(1)}, u32[]{:S(2)}, u32[]{:S(2)}) async-start(bf16[4,96,1024]{2,1,0:T(8,128)(2,1)} %add_convert_fusion), calls=%async_computation.3 | async-start | bytes 1572864 | tf_op jit(solution)/shard_map/all_to_all | solution.py:64
  135.3 1.1 copy-start.2
  137.7 19.8 %collective-permute-start = (bf16[96,4096]{1,0:T(8,128)(2,1)}, bf16[96,4096]{1,0:T(8,128)(2,1)}, u32[]{:S(2)}, u32[]{:S(2)}) collective-permute-start(bf16[96,4096]{1,0:T(8,128)(2,1)} %fusion.9), channel_id=1, source_target_pairs={{0,16},{16,0},{1,17},{17,1},{2,18},{18,2},{3,19},{19,3},{4,20},{20... | collective-permute-start | bytes 2359304 | tf_op jit(solution)/shard_map/ppermute | solution.py:19
where the time goes:
time: 161 us; the launch traced here: 160 us
  waiting for transfers between devices  70.7 us (44%)
  local copies, waits for them, and re-layouts  44.6 us (28%)
  starting transfers between devices  19.2 us (12%)
  other arithmetic  11.6 us (7%)
  matrix products  11.3 us (7%)
  between operations  2.2 us (1%)
    unnamed x14, local copies, waits for them, and re-layouts  24.7 us
    all_to_all x1, waiting for transfers between devices, per_device(): lax.all_to_all(keys[0, 0], 'seq', split_axis=2, concat_axis=1, tiled=True)  20 us
    all_to_all x1, waiting for transfers between devices, per_device(): lax.all_to_all(queries[0, 0], 'seq', split_axis=2, concat_axis=1, tiled=T...  20 us
    ppermute x1, waiting for transfers between devices, from_partner(): return lax.ppermute(block, axis, route)  13.1 us
    all_to_all x1, waiting for transfers between devices, per_device(): lax.all_to_all(combine(attended[0], attended[1]), 'seq', split_axis=0, co...  9.97 us
    dot_general x1, matrix products, one_block(): jnp.einsum('nhqk,nkhd->nqhd', weights, value_rows, preferred_element_type...  9.9 us
    all_to_all x1, waiting for transfers between devices, per_device(): lax.all_to_all(values[0, 0], 'seq', split_axis=2, concat_axis=1, tiled=True)  7.6 us
    all_to_all x1, local copies, waits for them, and re-layouts, per_device(): lax.all_to_all(keys[0, 0], 'seq', split_axis=2, concat_axis=1, tiled=True)  4.67 us
  transfers between devices with their start and end apart: 5, of which 5 were waited for; matrix products, arithmetic and copies ran while one was open for 19% of the time, Pallas kernels for 0%

commit v1 on v0

--- a/solution.py
+++ b/solution.py
@@ -56,7 +56,12 @@
 def per_device(queries, keys, values, latents, gain, steps_table, flags):
     attended = attend(
         (
-            lax.all_to_all(queries[0, 0], "seq", split_axis=2, concat_axis=1, tiled=True),
+            jnp.concatenate(
+                lax.all_to_all(
+                    jnp.stack(jnp.split(queries[0, 0], lax.axis_size("seq"), axis=2)), "seq", 0, 0
+                ),
+                axis=1,
+            ),
             lax.all_to_all(keys[0, 0], "seq", split_axis=2, concat_axis=1, tiled=True),
             lax.all_to_all(values[0, 0], "seq", split_axis=2, concat_axis=1, tiled=True),
         )

time: 161 us -> 156 us (0.969)
  waiting for transfers between devices: 70.7 us -> 66.1 us
  other arithmetic: 11.6 us -> 14.3 us
  local copies, waits for them, and re-layouts: 44.6 us -> 42.2 us
    all_to_all x1, waiting for transfers between devices: 20 us -> 16.1 us  [per_device(): lax.all_to_all(jnp.stack(jnp.split(queries[0, 0], lax.axis_size('seq'), a...]
    all_to_all x1 -> x0, local copies, waits for them, and re-layouts: 3.69 us -> none  [per_device(): lax.all_to_all(queries[0, 0], 'seq', split_axis=2, concat_axis=1, tiled=T...]
    unnamed x14 -> x21, local copies, waits for them, and re-layouts: 24.7 us -> 22.4 us
where the time goes in v1:
time: 156 us; the launch traced here: 155 us
  waiting for transfers between devices  66.1 us (42%)
  local copies, waits for them, and re-layouts  42.2 us (27%)
  starting transfers between devices  17.7 us (11%)
  other arithmetic  14.3 us (9%)
  matrix products  12.3 us (8%)
  between operations  2.19 us (1%)
    unnamed x21, local copies, waits for them, and re-layouts  22.4 us
    all_to_all x1, waiting for transfers between devices, per_device(): lax.all_to_all(keys[0, 0], 'seq', split_axis=2, concat_axis=1, tiled=True)  19.9 us
    all_to_all x1, waiting for transfers between devices, per_device(): lax.all_to_all(jnp.stack(jnp.split(queries[0, 0], lax.axis_size('seq'), a...  16.1 us
    ppermute x1, waiting for transfers between devices, from_partner(): return lax.ppermute(block, axis, route)  13.1 us
    dot_general x1, matrix products, one_block(): jnp.einsum('nhqk,nkhd->nqhd', weights, value_rows, preferred_element_type...  10.9 us
    all_to_all x1, waiting for transfers between devices, per_device(): lax.all_to_all(combine(attended[0], attended[1]), 'seq', split_axis=0, co...  9.97 us
    all_to_all x1, waiting for transfers between devices, per_device(): lax.all_to_all(values[0, 0], 'seq', split_axis=2, concat_axis=1, tiled=True)  6.94 us
    all_to_all x1, local copies, waits for them, and re-layouts, per_device(): lax.all_to_all(keys[0, 0], 'seq', split_axis=2, concat_axis=1, tiled=True)  6.07 us
  transfers between devices with their start and end apart: 5, of which 5 were waited for; matrix products, arithmetic and copies ran while one was open for 19% of the time, Pallas kernels for 0%

profile of v1, /device:TPU:0, one launch (start us, length us, event | category | flops | bytes accessed | tf_op | source)
XLA Modules:
  0.0 154.6 jit_solution(15284685113646394176)
XLA Ops:
  0.6 1.5 slice_bitcast_fusion.3
  2.2 1.3 pad_maximum_fusion
  3.5 4.4 %all-to-all-start = ((bf16[4,2,96,1024]{3,2,1,0:T(8,128)(2,1)}), bf16[4,2,96,1024]{3,2,1,0:T(8,128)(2,1)S(1)}, u32[]{:S(2)}, u32[]{:S(2)}) async-start(bf16[4,2,96,1024]{3,2,1,0:T(8,128)(2,1)} %pad_maximum_fusion), calls=%async_computation | async-start | bytes 3145728 | tf_op jit(solution)/shard_map/all_to_all | solution.py:60
  7.9 3.9 %copy.31 = bf16[1,1,2,96,4096]{3,2,4,1,0:T(2,128)(2,1)} copy(bf16[1,1,2,96,4096]{4,3,2,1,0:T(8,128)(2,1)S(1)} %copy-done.6) | data formatting | bytes 3145728 | tf_op args[1]
  11.8 16.1 %all-to-all-done = bf16[4,2,96,1024]{3,2,1,0:T(8,128)(2,1)S(1)} async-done(((bf16[4,2,96,1024]{3,2,1,0:T(8,128)(2,1)}), bf16[4,2,96,1024]{3,2,1,0:T(8,128)(2,1)S(1)}, u32[]{:S(2)}, u32[]{:S(2)}) %all-to-all-start) | async-done | bytes 1572896 | tf_op jit(solution)/shard_map/all_to_all | solution.py:60
  29.1 3.6 %all-to-all-start.1 = ((bf16[2,96,4096]{1,0,2:T(2,128)(2,1)}), bf16[2,96,4096]{1,0,2:T(2,128)(2,1)S(1)}, u32[]{:S(2)}, u32[]{:S(2)}) async-start(bf16[2,96,4096]{1,0,2:T(2,128)(2,1)} %bitcast.56), calls=%async_computation.1 | async-start | bytes 4194304 | tf_op jit(solution)/shard_map/all_to_all | solution.py:65
  32.7 5.7 %copy.35 = bf16[1,1,2,96,4096]{3,2,4,1,0:T(2,128)(2,1)} copy(bf16[1,1,2,96,4096]{4,3,2,1,0:T(8,128)(2,1)} %param.9) | data formatting | bytes 3145728 | tf_op args[2]
  38.4 19.9 %all-to-all-done.1 = bf16[2,96,4096]{1,0,2:T(2,128)(2,1)S(1)} async-done(((bf16[2,96,4096]{1,0,2:T(2,128)(2,1)}), bf16[2,96,4096]{1,0,2:T(2,128)(2,1)S(1)}, u32[]{:S(2)}, u32[]{:S(2)}) %all-to-all-start.1) | async-done | bytes 1572896 | tf_op jit(solution)/shard_map/all_to_all | solution.py:65
  58.3 1.3 copy-done.1
  59.7 3.6 %all-to-all-start.2 = ((bf16[2,96,4096]{1,0,2:T(2,128)(2,1)}), bf16[2,96,4096]{1,0,2:T(2,128)(2,1)S(1)}, u32[]{:S(2)}, u32[]{:S(2)}) async-start(bf16[2,96,4096]{1,0,2:T(2,128)(2,1)} %bitcast.10), calls=%async_computation.2 | async-start | bytes 4194304 | tf_op jit(solution)/shard_map/all_to_all | solution.py:66
  63.3 1.6 %copy.30 = bf16[2,4,96,1024]{3,2,1,0:T(8,128)(2,1)S(1)} copy(bf16[2,4,96,1024]{3,2,0,1:T(8,128)(2,1)} %bitcast.57) | data formatting | bytes 3145728 | tf_op jit(solution)/shard_map/reshape | solution.py:59
  64.9 1.6 %copy.45 = bf16[96,8,8,128]{3,2,1,0:T(8,128)(2,1)} copy(bf16[96,8,8,128]{3,1,2,0:T(8,128)(2,1)S(1)} %bitcast.61) | data formatting | bytes 3145728
  66.5 6.1 %copy.32 = bf16[2,96,4,1024]{3,1,2,0:T(8,128)(2,1)} copy(bf16[2,96,4,1024]{1,0,3,2:T(2,128)(2,1)} %bitcast.55) | data formatting | bytes 3145728 | tf_op jit(solution)/shard_map/all_to_all | solution.py:65
  72.6 2.0 %copy.46 = bf16[96,8,8,128]{3,2,1,0:T(8,128)(2,1)S(1)} copy(bf16[96,8,8,128]{3,1,2,0:T(8,128)(2,1)} %bitcast.62) | data formatting | bytes 3145728
  74.5 1.4 fusion.12
  76.0 3.6 %copy-done = f32[2,8,384,384]{2,3,1,0:T(8,128)} copy-done((f32[2,8,384,384]{2,3,1,0:T(8,128)}, f32[2,8,384,384]{2,3,1,0:T(8,128)S(1)}, u32[]{:S(2)}) %copy-start) | copy-done | bytes 9437208
  79.6 2.4 %fusion.26 = f32[2,8,384]{2,1,0:T(8,128)S(1)} fusion(f32[2,8,384,384]{2,3,1,0:T(8,128)S(1)} %fusion.12), kind=kOutput, calls=%fused_computation.35 | output fusion | flops 9437567 | bytes 9461760 | tf_op jit(solution)/shard_map/while/body/eval_jaxpr/sub | solution.py:47
  82.0 6.9 %all-to-all-done.2 = bf16[2,96,4096]{1,0,2:T(2,128)(2,1)S(1)} async-done(((bf16[2,96,4096]{1,0,2:T(2,128)(2,1)}), bf16[2,96,4096]{1,0,2:T(2,128)(2,1)S(1)}, u32[]{:S(2)}, u32[]{:S(2)}) %all-to-all-start.2) | async-done | bytes 1572896 | tf_op jit(solution)/shard_map/all_to_all | solution.py:66
  88.9 3.7 %copy.36 = bf16[2,96,4,1024]{3,1,2,0:T(8,128)(2,1)} copy(bf16[2,96,4,1024]{1,0,3,2:T(2,128)(2,1)S(1)} %bitcast.54) | data formatting | bytes 3145728 | tf_op jit(solution)/shard_map/all_to_all | solution.py:66
  92.7 1.8 %copy.47 = bf16[96,8,8,128]{3,2,1,0:T(8,128)(2,1)S(1)} copy(bf16[96,8,8,128]{3,1,2,0:T(8,128)(2,1)} %bitcast.63) | data formatting | bytes 3145728
  94.5 10.9 %fusion.15 = bf16[2,384,8,128]{3,1,2,0:T(8,128)(2,1)} fusion(bf16[2,384,8,128]{3,2,1,0:T(8,128)(2,1)S(1)} %bitcast.65, f32[2,8,384]{2,1,0:T(8,128)S(1)} %fusion.26, f32[2,8,384,384]{2,3,1,0:T(8,128)} %copy-done), kind=kOutput, calls=%fused_computation.23 | convolution fusion | flops 616569216 | bytes 12607488 | tf_op jit(solution)/shard_map/while/body/eval_jaxpr/nhqk,nkhd->nqhd/dot_general | solution.py:48
  105.4 1.6 %slice_convert_fusion = (f32[1,384,8,128]{3,1,2,0:T(8,128)S(1)}, f32[1,384,8,128]{3,1,2,0:T(8,128)S(1)}) fusion(bf16[2,384,8,128]{3,1,2,0:T(8,128)(2,1)} %fusion.15), kind=kLoop, calls=%fused_computation.24 | loop fusion | flops 786432 | bytes 4718592 | tf_op jit(solution)/shard_map/convert_element_type | solution.py:29
  107.9 1.4 reshape.132
  110.2 1.4 reshape.133
  112.1 2.6 %add_convert_fusion = bf16[4,96,1024]{2,1,0:T(8,128)(2,1)} fusion(f32[4,96,1024]{2,1,0:T(8,128)S(1)} %copy-done.4, f32[4,96,1024]{2,1,0:T(8,128)} %reshape.133), kind=kLoop, calls=%fused_computation.22 | loop fusion | flops 1572864 | bytes 3932160 | tf_op jit(solution)/shard_map/convert_element_type | solution.py:29
  114.8 3.8 %all-to-all-start.3 = ((bf16[4,96,1024]{2,1,0:T(8,128)(2,1)}), bf16[4,96,1024]{2,1,0:T(8,128)(2,1)S(1)}, u32[]{:S(2)}, u32[]{:S(2)}) async-start(bf16[4,96,1024]{2,1,0:T(8,128)(2,1)} %add_convert_fusion), calls=%async_computation.3 | async-start | bytes 1572864 | tf_op jit(solution)/shard_map/all_to_all | solution.py:69
  120.0 10.0 %all-to-all-done.3 = bf16[4,96,1024]{2,1,0:T(8,128)(2,1)S(1)} async-done(((bf16[4,96,1024]{2,1,0:T(8,128)(2,1)}), bf16[4,96,1024]{2,1,0:T(8,128)(2,1)S(1)}, u32[]{:S(2)}, u32[]{:S(2)}) %all-to-all-start.3) | async-done | bytes 786464 | tf_op jit(solution)/shard_map/all_to_all | solution.py:69
  131.5 1.2 fusion.9
  132.8 2.2 %collective-permute-start = (bf16[96,4096]{1,0:T(8,128)(2,1)}, bf16[96,4096]{1,0:T(8,128)(2,1)}, u32[]{:S(2)}, u32[]{:S(2)}) collective-permute-start(bf16[96,4096]{1,0:T(8,128)(2,1)} %fusion.9), channel_id=1, source_target_pairs={{0,16},{16,0},{1,17},{17,1},{2,18},{18,2},{3,19},{19,3},{4,20},{20... | collective-permute-start | bytes 2359304 | tf_op jit(solution)/shard_map/ppermute | solution.py:19
  137.1 2.4 %fusion.7 = bf16[1,1,96,4096]{3,2,1,0:T(8,128)(2,1)} fusion(bf16[1,1,96,4096]{3,2,1,0:T(8,128)(2,1)} %param.10, f32[1,1,96,4096]{3,2,1,0:T(8,128)S(1)} %reshape.134, f32[4096]{0:T(1024)S(1)} %bitcast.67, f32[96]{0:T(128)S(1)} %add_rsqrt_fusion, f32[]{:T(128)} %bitcast), kind=kLoop, calls=%fused_computation.13 | loop fusion | flops 2359296 | bytes 3162500 | tf_op jit(solution)/shard_map/convert_element_type | solution.py:79
  139.5 13.1 %collective-permute-done = bf16[96,4096]{1,0:T(8,128)(2,1)} collective-permute-done((bf16[96,4096]{1,0:T(8,128)(2,1)}, bf16[96,4096]{1,0:T(8,128)(2,1)}, u32[]{:S(2)}, u32[]{:S(2)}) %collective-permute-start) | collective-permute-done | bytes 786464 | tf_op jit(solution)/shard_map/ppermute | solution.py:19
  152.6 2.1 %select_bitcast_fusion = bf16[1,1,96,4096]{3,2,1,0:T(8,128)(2,1)} fusion(bf16[96,4096]{1,0:T(8,128)(2,1)} %collective-permute-done, bf16[96,4096]{1,0:T(8,128)(2,1)} %fusion.9, pred[]{:T(512)} %bitcast.16), kind=kLoop, calls=%fused_computation.26 | loop fusion | flops 393216 | bytes 2359297 | tf_op jit(solution)/shard_map/broadcast_in_dim | solution.py:83
  (23 shorter events, 7.1 us)
Async XLA Ops:
  3.5 4.4 %copy-start.6 = (bf16[1,1,2,96,4096]{4,3,2,1,0:T(8,128)(2,1)S(1)}, bf16[1,1,2,96,4096]{4,3,2,1,0:T(8,128)(2,1)}, u32[]{:S(2)}) copy-start(bf16[1,1,2,96,4096]{4,3,2,1,0:T(8,128)(2,1)} %param.8) | copy-start | bytes 4718596
  3.5 24.4 %all-to-all-start = ((bf16[4,2,96,1024]{3,2,1,0:T(8,128)(2,1)}), bf16[4,2,96,1024]{3,2,1,0:T(8,128)(2,1)S(1)}, u32[]{:S(2)}, u32[]{:S(2)}) async-start(bf16[4,2,96,1024]{3,2,1,0:T(8,128)(2,1)} %pad_maximum_fusion), calls=%async_computation | async-start | bytes 3145728 | tf_op jit(solution)/shard_map/all_to_all | solution.py:60
  28.0 1.1 copy-start.2
  29.1 29.2 %all-to-all-start.1 = ((bf16[2,96,4096]{1,0,2:T(2,128)(2,1)}), bf16[2,96,4096]{1,0,2:T(2,128)(2,1)S(1)}, u32[]{:S(2)}, u32[]{:S(2)}) async-start(bf16[2,96,4096]{1,0,2:T(2,128)(2,1)} %bitcast.56), calls=%async_computation.1 | async-start | bytes 4194304 | tf_op jit(solution)/shard_map/all_to_all | solution.py:65
  58.3 1.3 copy-start.1
  59.7 29.2 %all-to-all-start.2 = ((bf16[2,96,4096]{1,0,2:T(2,128)(2,1)}), bf16[2,96,4096]{1,0,2:T(2,128)(2,1)S(1)}, u32[]{:S(2)}, u32[]{:S(2)}) async-start(bf16[2,96,4096]{1,0,2:T(2,128)(2,1)} %bitcast.10), calls=%async_computation.2 | async-start | bytes 4194304 | tf_op jit(solution)/shard_map/all_to_all | solution.py:66
  72.6 2.0 %copy-start.3 = (bf16[96,8,8,128]{3,2,1,0:T(8,128)(2,1)S(1)}, bf16[96,8,8,128]{3,2,1,0:T(8,128)(2,1)}, u32[]{:S(2)}) copy-start(bf16[96,8,8,128]{3,2,1,0:T(8,128)(2,1)} %copy.45) | copy-start | bytes 4718596
  75.9 3.6 %copy-start = (f32[2,8,384,384]{2,3,1,0:T(8,128)}, f32[2,8,384,384]{2,3,1,0:T(8,128)S(1)}, u32[]{:S(2)}) copy-start(f32[2,8,384,384]{2,3,1,0:T(8,128)S(1)} %fusion.12) | copy-start | bytes 28311556
  110.2 1.9 %copy-start.4 = (f32[4,96,1024]{2,1,0:T(8,128)S(1)}, f32[4,96,1024]{2,1,0:T(8,128)}, u32[]{:S(2)}) copy-start(f32[4,96,1024]{2,1,0:T(8,128)} %reshape.132) | copy-start | bytes 4718596
  114.8 4.5 %copy-start.7 = (bf16[1,4096]{1,0:T(2,128)(2,1)S(1)}, bf16[1,4096]{1,0:T(2,128)(2,1)}, u32[]{:S(2)}) copy-start(bf16[1,4096]{1,0:T(2,128)(2,1)} %param.11) | copy-start | bytes 24580
  114.8 15.2 %all-to-all-start.3 = ((bf16[4,96,1024]{2,1,0:T(8,128)(2,1)}), bf16[4,96,1024]{2,1,0:T(8,128)(2,1)S(1)}, u32[]{:S(2)}, u32[]{:S(2)}) async-start(bf16[4,96,1024]{2,1,0:T(8,128)(2,1)} %add_convert_fusion), calls=%async_computation.3 | async-start | bytes 1572864 | tf_op jit(solution)/shard_map/all_to_all | solution.py:69
  130.4 1.1 copy-start.5
  132.8 19.8 %collective-permute-start = (bf16[96,4096]{1,0:T(8,128)(2,1)}, bf16[96,4096]{1,0:T(8,128)(2,1)}, u32[]{:S(2)}, u32[]{:S(2)}) collective-permute-start(bf16[96,4096]{1,0:T(8,128)(2,1)} %fusion.9), channel_id=1, source_target_pairs={{0,16},{16,0},{1,17},{17,1},{2,18},{18,2},{3,19},{19,3},{4,20},{20... | collective-permute-start | bytes 2359304 | tf_op jit(solution)/shard_map/ppermute | solution.py:19
